TPU v7x, 32 devices: a whole 2x2x4 slice. The times are simulated.
32 devices in a mesh: grp: 2 (over core), row: 4 (over z), col: 4 (over y, x).
Axes of the slice: x: 2, y: 2, z: 4, core: 2. Of those that a mesh axis runs over, the one named last changes fastest.
Arguments:
- ainv_anc: bfloat16 [6144, 6144], P(('grp', 'row'), 'col'), may hold values from -12 to 12
- l_upper: bfloat16 [6144, 1024], P(('grp', 'row'), 'col'), may hold values from -0.078125 to 0.078125
- mask_upper: int32 [4, 24], replicated, may hold values from 0 to 1, as said below
- dinv_upper: float32 [256, 1024], P(None, 'col'), may hold values from -6 to 6
- l_lower: bfloat16 [6144, 1024], P(('grp', 'row'), 'col'), may hold values from -0.078125 to 0.078125
- mask_lower: int32 [4, 24], replicated, may hold values from 0 to 1, as said below
- parent: int32 [4], replicated, may hold values from 0 to 3
- lp_lower: bfloat16 [256, 1024], P(None, 'col'), may hold values from -0.375 to 0.375
- dinv_lower: float32 [256, 1024], P(None, 'col'), may hold values from -6 to 6
Outputs:
- x_upper: bfloat16 [6144, 1024], P(('grp', 'row'), 'col')
- diag_upper: bfloat16 [256, 1024], P(None, 'col')
- y_lower: bfloat16 [6144, 1024], P(('grp', 'row'), 'col')
- y_parent: bfloat16 [256, 1024], P(None, 'col')
- diag_lower: bfloat16 [256, 1024], P(None, 'col')
Inputs may be any that keep to these rules, and one draw needn't show every extreme that they name: mask_upper[u, a] is 1 where ancestor block a lies in the structure of upper supernode u. mask_lower[l, a] is 1 where ancestor block a lies in the structure of lower supernode l. parent[l] is the upper supernode whose columns hold lower supernode l's parent block.
All inputs are finite; a program needn't handle non-finite values.
Results may differ from a plain program's by a relative error of at most 0.0095.
Values may be sent and summed in bfloat16 or wider, within the bound.
A program may use at most 128 MiB of HBM per device.

v0:
```python
import jax
import jax.numpy as jnp
from jax import lax
from jax.sharding import PartitionSpec as P

B = 256


def masked_shard(factor, pattern, block_from, node_from):
    height, breadth = factor.shape
    blocks = height // B
    supernodes = breadth // B
    picked = lax.dynamic_slice(pattern, (node_from, block_from), (supernodes, blocks))
    shaped = factor.reshape(blocks, B, supernodes, B)
    keeping = (jnp.transpose(picked) > 0)[:, None, :, None]
    return jnp.where(keeping, shaped, jnp.zeros((), factor.dtype)).reshape(height, breadth)


def column_panel(masked):
    every_row = lax.all_gather(masked, ("grp", "row"), axis=0, tiled=True)
    gathered = lax.all_to_all(every_row, "col", split_axis=0, concat_axis=1, tiled=True)
    return gathered


def summed_panel(ancestor, masked):
    gathered = column_panel(masked)
    partial_value = jnp.dot(ancestor, gathered, preferred_element_type=jnp.float32)
    return lax.psum_scatter(partial_value, "col", scatter_dimension=1, tiled=True)


def on_device(
    ainv_anc, l_upper, mask_upper, dinv_upper, l_lower, mask_lower, parent, lp_lower, dinv_lower
):
    height = ainv_anc.shape[0]
    breadth = l_upper.shape[1]
    per_device = breadth // B
    block_from = lax.axis_index(("grp", "row")) * (height // B)
    node_from = lax.axis_index("col") * per_device
    upper_masked = masked_shard(l_upper, mask_upper, block_from, node_from)
    x_upper = (-summed_panel(ainv_anc, upper_masked)).astype(jnp.bfloat16)
    upper_terms = jnp.einsum(
        "akb,akc->bkc",
        upper_masked.reshape(height, per_device, B),
        x_upper.reshape(height, per_device, B),
        preferred_element_type=jnp.float32,
    ).reshape(B, breadth)
    upper_total = lax.psum(upper_terms, ("grp", "row"))
    diag_upper = (dinv_upper - upper_total).astype(jnp.bfloat16)
    lower_masked = masked_shard(l_lower, mask_lower, block_from, node_from)
    lower_sum = summed_panel(ainv_anc, lower_masked)
    x_rows, diag_rows = (
        lax.all_gather(x_upper, "col", axis=1, tiled=True),
        lax.all_gather(diag_upper, "col", axis=1, tiled=True),
    )
    parents_here = lax.dynamic_slice_in_dim(parent, node_from, per_device)
    lower_parts, crossed_parts, own_parts = ([], [], [])
    member = 0
    chosen = lax.dynamic_slice_in_dim(x_rows, parents_here[member] * B, B, 1)
    coupling = jnp.dot(chosen, lp_lower, preferred_element_type=jnp.float32)
    y_block = (-(lower_sum + coupling)).astype(jnp.bfloat16)
    lower_parts.append(y_block)
    crossed_parts.append(
        jnp.einsum("ab,ac->bc", chosen, lower_masked, preferred_element_type=jnp.float32)
    )
    own_parts.append(
        jnp.einsum("ab,ac->bc", lower_masked, y_block, preferred_element_type=jnp.float32)
    )
    y_lower = lower_parts[0]
    crossed_sum, own_sum = lax.psum((crossed_parts[0], own_parts[0]), ("grp", "row"))
    parent_parts, diag_parts = ([], [])
    member = 0
    parent_diag = lax.dynamic_slice_in_dim(diag_rows, parents_here[member] * B, B, 1)
    parent_terms = jnp.dot(parent_diag, lp_lower, preferred_element_type=jnp.float32)
    y_block = (-(crossed_sum + parent_terms)).astype(jnp.bfloat16)
    back_terms = jnp.einsum("cb,cd->bd", lp_lower, y_block, preferred_element_type=jnp.float32)
    diag_block = dinv_lower - own_sum - back_terms
    parent_parts.append(y_block)
    diag_parts.append(diag_block.astype(jnp.bfloat16))
    y_parent = parent_parts[0]
    diag_lower = diag_parts[0]
    return (x_upper, diag_upper, y_lower, y_parent, diag_lower)


def solution(mesh):
    return jax.shard_map(
        on_device,
        mesh=mesh,
        in_specs=(
            P(("grp", "row"), "col"),
            P(("grp", "row"), "col"),
            P(),
            P(None, "col"),
            P(("grp", "row"), "col"),
            P(),
            P(),
            P(None, "col"),
            P(None, "col"),
        ),
        out_specs=(
            P(("grp", "row"), "col"),
            P(None, "col"),
            P(("grp", "row"), "col"),
            P(None, "col"),
            P(None, "col"),
        ),
        check_vma=False,
    )
```

profile of v0, /device:TPU:0, one launch (start us, length us, event | category | flops | bytes accessed | tf_op | source)
XLA Modules:
  0.0 344.0 jit_solution(8300862386639493324)
XLA Ops:
  7.2 0.0 copy-start
  7.2 0.0 all-gather.4.cloned.1.call-start
  7.2 0.9 compare_bitcast_fusion
  8.2 0.1 broadcast_in_dim.28
  8.3 1.9 broadcast_select_fusion.1
  10.2 0.0 all-gather.4.cloned.1.call-update
  10.2 0.0 all-gather.6.cloned.1.call-start
  10.2 0.1 broadcast_in_dim.32
  10.3 1.9 broadcast_select_fusion
  12.3 0.0 all-gather.6.cloned.1.call-update
  12.3 0.0 reduce-scatter.3.cloned.1.call-start
  12.3 39.0 %all-gather.4.cloned.1.call-done = bf16[6144,256]{1,0:T(8,128)(2,1)} async-done(((bf16[768,256]{1,0:T(8,128)(2,1)}), bf16[6144,256]{1,0:T(8,128)(2,1)}) %all-gather.4.cloned.1.call-update) | async-done | bytes 3145744 | tf_op jit(solution)/shard_map/all_gather | solution.py:20
  51.3 42.6 %all_to_all.38 = bf16[4,1536,256]{2,1,0:T(8,128)(2,1)} all-to-all(bf16[4,1536,256]{2,1,0:T(8,128)(2,1)} %bitcast.43), channel_id=1, replica_groups=mesh['grp'=2,'row'=4,'col'=4] {'col'}, dimensions={0} | all-to-all | bytes 6291456 | tf_op jit(solution)/shard_map/all_to_all | solution.py:21
  93.9 4.6 %copy.26 = bf16[1536,4,256]{0,2,1:T(8,128)(2,1)} copy(bf16[1536,4,256]{2,0,1:T(8,128)(2,1)} %bitcast.40) | data formatting | bytes 6291456 | tf_op jit(solution)/shard_map/all_to_all | solution.py:21
  98.5 0.0 copy-done
  98.5 6.2 %convolution_bitcast_fusion.1 = f32[768,1024]{0,1:T(8,128)} fusion(bf16[1536,1024]{0,1:T(8,128)(2,1)} %bitcast.44, bf16[768,1536]{1,0:T(8,128)(2,1)S(1)} %copy-done), kind=kOutput, calls=%fused_computation.1 | convolution fusion | flops 2415919104 | bytes 8650752 | tf_op jit(solution)/shard_map/dot_general | solution.py:27
  104.7 0.0 reduce-scatter.3.cloned.1.call-update
  104.7 0.0 reduce-scatter.5.cloned.1.call-start
  104.8 0.0 all-gather.6.cloned.1.call-done
  104.8 57.3 %all_to_all.39 = bf16[4,1536,256]{2,1,0:T(8,128)(2,1)} all-to-all(bf16[4,1536,256]{2,1,0:T(8,128)(2,1)} %bitcast.42), channel_id=1, replica_groups=mesh['grp'=2,'row'=4,'col'=4] {'col'}, dimensions={0} | all-to-all | bytes 6291456 | tf_op jit(solution)/shard_map/all_to_all | solution.py:21
  162.1 4.6 %copy.28 = bf16[1536,4,256]{0,2,1:T(8,128)(2,1)} copy(bf16[1536,4,256]{2,0,1:T(8,128)(2,1)} %bitcast.41) | data formatting | bytes 6291456 | tf_op jit(solution)/shard_map/all_to_all | solution.py:21
  166.7 6.3 %convolution_bitcast_fusion = f32[768,1024]{0,1:T(8,128)} fusion(bf16[1536,1024]{0,1:T(8,128)(2,1)} %bitcast.45, bf16[768,1536]{1,0:T(8,128)(2,1)S(1)} %copy-done), kind=kOutput, calls=%fused_computation | convolution fusion | flops 2415919104 | bytes 8650752 | tf_op jit(solution)/shard_map/dot_general | solution.py:27
  173.0 0.0 reduce-scatter.5.cloned.1.call-update
  173.0 0.0 all-gather.8.cloned.1.call-start
  173.1 5.7 %reduce-scatter.3.cloned.1.call-done = f32[768,256]{0,1:T(8,128)} async-done(((f32[768,1024]{0,1:T(8,128)}), f32[768,256]{0,1:T(8,128)}) %reduce-scatter.3.cloned.1.call-update) | async-done | bytes 786448 | tf_op jit(solution)/shard_map/reduce_scatter | solution.py:28
  178.8 1.9 negate_convert_fusion
  180.7 0.0 all-gather.8.cloned.1.call-update
  180.7 0.0 copy-start.2
  180.7 0.0 all-reduce.3.cloned.1.call-start
  180.8 0.6 dynamic_slice.17
  182.1 2.0 convolution_bitcast_fusion.2
  184.0 41.5 %reduce-scatter.5.cloned.1.call-done = f32[768,256]{0,1:T(8,128)} async-done(((f32[768,1024]{0,1:T(8,128)}), f32[768,256]{0,1:T(8,128)}) %reduce-scatter.5.cloned.1.call-update) | async-done | bytes 786448 | tf_op jit(solution)/shard_map/reduce_scatter | solution.py:28
  225.6 33.1 %all-gather.8.cloned.1.call-done = bf16[768,1024]{0,1:T(8,128)(2,1)} async-done(((bf16[768,256]{0,1:T(8,128)(2,1)}), bf16[768,1024]{0,1:T(8,128)(2,1)}) %all-gather.8.cloned.1.call-update) | async-done | bytes 1572880 | tf_op jit(solution)/shard_map/all_gather | solution.py:52
  258.7 1.6 fusion.1
  260.3 1.0 fusion.13
  261.3 2.0 fusion.6
  263.3 0.0 all-reduce.3.cloned.1.call-update
  263.4 1.8 copy.27
  265.2 0.9 copy.31
  266.1 0.9 copy.33
  267.0 54.4 %all-reduce.3.cloned.1.call-done = (f32[256,256]{0,1:T(8,128)}, f32[256,256]{1,0:T(8,128)}, f32[256,256]{1,0:T(8,128)}) async-done(((f32[256,256]{0,1:T(8,128)}, f32[256,256]{1,0:T(8,128)}, f32[256,256]{1,0:T(8,128)}), (f32[256,256]{0,1:T(8,128)}, f32[256,256]{1,0:T(8,128)}, f32[256,256]{1,0:T(8,128)})) %all-reduce.3.cloned.1.call-update) | async-done | bytes 786448 | tf_op jit(solution)/shard_map/psum | solution.py:47
  321.4 1.1 subtract_convert_fusion
  322.5 0.8 copy.32
  323.3 10.7 %all_gather.15 = bf16[256,1024]{0,1:T(8,128)(2,1)S(1)} all-gather(bf16[256,256]{0,1:T(8,128)(2,1)S(1)} %subtract_convert_fusion), channel_id=1, replica_groups=mesh['grp'=2,'row'=4,'col'=4] {'col'}, dimensions={1}, use_global_device_ids=true | all-gather | bytes 655360 | tf_op jit(solution)/shard_map/all_gather | solution.py:53
  333.9 1.2 fusion.5
  335.2 0.0 copy-start.5
  335.2 2.0 fusion.4
  337.2 0.0 copy-done.5
  (11 shorter events, 0.1 us)
Async XLA Ops:
  7.2 91.4 %copy-start = (bf16[768,1536]{1,0:T(8,128)(2,1)S(1)}, bf16[768,1536]{1,0:T(8,128)(2,1)}, u32[]{:S(2)}) copy-start(bf16[768,1536]{1,0:T(8,128)(2,1)} %param.9) | copy-start | bytes 7077892
  7.2 44.1 %all-gather.4.cloned.1.call-start = ((), (), s32[]{:S(2)}) async-start(), calls=%async_computation.4 | async-start | bytes 3538944 | tf_op jit(solution)/shard_map/all_gather | solution.py:20
  10.2 94.6 %all-gather.6.cloned.1.call-start = ((), (), s32[]{:S(2)}) async-start(), calls=%async_computation.6 | async-start | bytes 3538944 | tf_op jit(solution)/shard_map/all_gather | solution.py:20
  12.3 166.5 %reduce-scatter.3.cloned.1.call-start = ((), (), s32[]{:S(2)}) async-start(), calls=%async_computation.5 | async-start | bytes 3932160 | tf_op jit(solution)/shard_map/reduce_scatter | solution.py:28
  104.7 120.8 %reduce-scatter.5.cloned.1.call-start = ((), (), s32[]{:S(2)}) async-start(), calls=%async_computation.7 | async-start | bytes 3932160 | tf_op jit(solution)/shard_map/reduce_scatter | solution.py:28
  173.0 7.8 %copy-start.6 = (s32[4]{0:T(128)S(1)}, s32[4]{0:T(128)}, u32[]{:S(2)}) copy-start(s32[4]{0:T(128)} %param.15) | copy-start | bytes 52
  173.0 9.0 %copy-start.3 = (bf16[768,256]{1,0:T(8,128)(2,1)S(1)}, bf16[768,256]{1,0:T(8,128)(2,1)}, u32[]{:S(2)}) copy-start(bf16[768,256]{1,0:T(8,128)(2,1)} %broadcast_select_fusion.1) | copy-start | bytes 1179652
  173.0 87.3 %copy-start.1 = (bf16[768,256]{1,0:T(8,128)(2,1)S(1)}, bf16[768,256]{1,0:T(8,128)(2,1)}, u32[]{:S(2)}) copy-start(bf16[768,256]{1,0:T(8,128)(2,1)} %broadcast_select_fusion) | copy-start | bytes 1179652
  173.0 85.6 %all-gather.8.cloned.1.call-start = ((), (), s32[]{:S(2)}) async-start(), calls=%async_computation.8 | async-start | bytes 1966080 | tf_op jit(solution)/shard_map/all_gather | solution.py:52
  180.7 84.5 %copy-start.2 = (bf16[768,256]{0,1:T(8,128)(2,1)S(1)}, bf16[768,256]{0,1:T(8,128)(2,1)}, u32[]{:S(2)}) copy-start(bf16[768,256]{0,1:T(8,128)(2,1)} %negate_convert_fusion) | copy-start | bytes 1179652
  180.7 140.7 %all-reduce.3.cloned.1.call-start = ((), (), s32[]{:S(2)}) async-start(), calls=%async_computation.9 | async-start | bytes 1572864 | tf_op jit(solution)/shard_map/psum | solution.py:47
  263.3 71.9 %copy-start.4 = (bf16[256,256]{1,0:T(8,128)(2,1)S(1)}, bf16[256,256]{1,0:T(8,128)(2,1)}, u32[]{:S(2)}) copy-start(bf16[256,256]{1,0:T(8,128)(2,1)} %param.16) | copy-start | bytes 393220
  335.2 2.0 copy-start.5
Sparse Core Ops, SparseCore 0:
  10.3 40.9 all-gather.3
  52.9 37.1 all-gather.5
  104.9 73.8 reduce-scatter.2
  181.6 43.8 reduce-scatter.4
  227.8 30.8 all-gather.7
  263.5 57.9 all-reduce.2
where the time goes:
time: 345 us; the launch traced here: 344 us
  waiting for transfers between devices  174 us (50%)
  blocking collectives  111 us (32%)
  matrix products  22.3 us (6%)
  between operations  14.9 us (4%)
  local copies, waits for them, and re-layouts  14.5 us (4%)
  other arithmetic  7.74 us (2%)
    all_to_all x2, blocking collectives, column_panel(): lax.all_to_all(every_row, 'col', split_axis=0, concat_axis=1, tiled=True)  99.9 us
    psum x1, waiting for transfers between devices, on_device(): upper_total = lax.psum(upper_terms, ('grp', 'row'))  54.4 us
    reduce_scatter x2, waiting for transfers between devices, summed_panel(): lax.psum_scatter(partial_value, 'col', scatter_dimension=1, tiled=True)  47.2 us
    all_gather x2, waiting for transfers between devices, column_panel(): every_row = lax.all_gather(masked, ('grp', 'row'), axis=0, tiled=True)  39 us
    all_gather x1, waiting for transfers between devices, on_device(): lax.all_gather(x_upper, 'col', axis=1, tiled=True)  33.1 us
    dot_general x2, matrix products, summed_panel(): jnp.dot(ancestor, gathered, preferred_element_type=jnp.float32)  12.5 us
    all_gather x1, blocking collectives, on_device(): lax.all_gather(diag_upper, 'col', axis=1, tiled=True)  10.7 us
    all_to_all x2, local copies, waits for them, and re-layouts, column_panel(): lax.all_to_all(every_row, 'col', split_axis=0, concat_axis=1, tiled=True)  9.26 us
  transfers between devices with their start and end apart: 6, of which 5 were waited for; matrix products, arithmetic and copies ran while one was open for 9% of the time, Pallas kernels for 0%

commit v1 on v0

--- a/solution.py
+++ b/solution.py
@@ -44,7 +44,9 @@
         x_upper.reshape(height, per_device, B),
         preferred_element_type=jnp.float32,
     ).reshape(B, breadth)
-    upper_total = lax.psum(upper_terms, ("grp", "row"))
+    upper_total = upper_terms
+    for k0 in ("row", "grp"):
+        upper_total = lax.psum(upper_total, axis_name=k0)
     diag_upper = (dinv_upper - upper_total).astype(jnp.bfloat16)
     lower_masked = masked_shard(l_lower, mask_lower, block_from, node_from)
     lower_sum = summed_panel(ainv_anc, lower_masked)

time: 345 us -> 388 us (1.12)
  waiting for transfers between devices: 174 us -> 218 us
    psum x1 -> x3, waiting for transfers between devices: 54.4 us -> 87.7 us  [the longest x1 45.8 us: on_device(): lax.psum((crossed_parts[0], own_parts[0]), ('grp', 'row'))]
    reduce_scatter x2, waiting for transfers between devices: 47.2 us -> 58.5 us  [summed_panel(): lax.psum_scatter(partial_value, 'col', scatter_dimension=1, tiled=True)]
  transfers between devices with their start and end apart: 6 -> 8, of which waited for: 5 -> 7; matrix products, arithmetic and copies ran while one was open for 9% -> 9% of each run, Pallas kernels for 0% -> 0%
where the time goes in v1:
time: 388 us; the launch traced here: 387 us
  waiting for transfers between devices  218 us (56%)
  blocking collectives  112 us (29%)
  matrix products  21.2 us (5%)
  between operations  14.9 us (4%)
  local copies, waits for them, and re-layouts  13.8 us (4%)
  other arithmetic  6.94 us (2%)
    all_to_all x2, blocking collectives, column_panel(): lax.all_to_all(every_row, 'col', split_axis=0, concat_axis=1, tiled=True)  99.9 us
    reduce_scatter x2, waiting for transfers between devices, summed_panel(): lax.psum_scatter(partial_value, 'col', scatter_dimension=1, tiled=True)  58.5 us
    psum x1, waiting for transfers between devices, on_device(): lax.psum((crossed_parts[0], own_parts[0]), ('grp', 'row'))  45.8 us
    psum x2, waiting for transfers between devices, on_device(): upper_total = lax.psum(upper_total, axis_name=k0)  42 us
    all_gather x2, waiting for transfers between devices, column_panel(): every_row = lax.all_gather(masked, ('grp', 'row'), axis=0, tiled=True)  38.9 us
    all_gather x1, waiting for transfers between devices, on_device(): lax.all_gather(x_upper, 'col', axis=1, tiled=True)  32.6 us
    dot_general x2, matrix products, summed_panel(): jnp.dot(ancestor, gathered, preferred_element_type=jnp.float32)  12.4 us
    all_gather x1, blocking collectives, on_device(): lax.all_gather(diag_upper, 'col', axis=1, tiled=True)  11.7 us
  transfers between devices with their start and end apart: 8, of which 7 were waited for; matrix products, arithmetic and copies ran while one was open for 9% of the time, Pallas kernels for 0%

profile of v1, /device:TPU:0, one launch (start us, length us, event | category | flops | bytes accessed | tf_op | source)
XLA Modules:
  0.0 387.1 jit_solution(417148724091128572)
XLA Ops:
  7.2 0.0 all-gather.4.cloned.1.call-start
  7.2 0.9 compare_bitcast_fusion
  8.2 0.1 broadcast_in_dim.28
  8.3 1.9 broadcast_select_fusion.1
  10.2 0.0 all-gather.4.cloned.1.call-update
  10.2 0.0 all-gather.6.cloned.1.call-start
  10.2 0.1 broadcast_in_dim.32
  10.3 1.9 broadcast_select_fusion
  12.3 0.0 all-gather.6.cloned.1.call-update
  12.3 0.0 reduce-scatter.3.cloned.1.call-start
  12.4 38.9 %all-gather.4.cloned.1.call-done = bf16[6144,256]{1,0:T(8,128)(2,1)} async-done(((bf16[768,256]{1,0:T(8,128)(2,1)}), bf16[6144,256]{1,0:T(8,128)(2,1)}) %all-gather.4.cloned.1.call-update) | async-done | bytes 3145744 | tf_op jit(solution)/shard_map/all_gather | solution.py:20
  51.3 42.6 %all_to_all.38 = bf16[4,1536,256]{2,1,0:T(8,128)(2,1)} all-to-all(bf16[4,1536,256]{2,1,0:T(8,128)(2,1)} %bitcast.43), channel_id=1, replica_groups=mesh['grp'=2,'row'=4,'col'=4] {'col'}, dimensions={0} | all-to-all | bytes 6291456 | tf_op jit(solution)/shard_map/all_to_all | solution.py:21
  93.9 4.6 %copy.26 = bf16[1536,4,256]{0,2,1:T(8,128)(2,1)} copy(bf16[1536,4,256]{2,0,1:T(8,128)(2,1)} %bitcast.40) | data formatting | bytes 6291456 | tf_op jit(solution)/shard_map/all_to_all | solution.py:21
  98.5 6.2 %convolution_bitcast_fusion.1 = f32[768,1024]{0,1:T(8,128)} fusion(bf16[1536,1024]{0,1:T(8,128)(2,1)} %bitcast.45, bf16[768,1536]{1,0:T(8,128)(2,1)S(1)} %copy-done), kind=kOutput, calls=%fused_computation.1 | convolution fusion | flops 2415919104 | bytes 8650752 | tf_op jit(solution)/shard_map/dot_general | solution.py:27
  104.7 0.0 reduce-scatter.3.cloned.1.call-update
  104.8 0.0 all-reduce.5.cloned.1.call-start
  104.8 0.0 all-gather.6.cloned.1.call-done
  104.8 57.3 %all_to_all.39 = bf16[4,1536,256]{2,1,0:T(8,128)(2,1)} all-to-all(bf16[4,1536,256]{2,1,0:T(8,128)(2,1)} %bitcast.42), channel_id=1, replica_groups=mesh['grp'=2,'row'=4,'col'=4] {'col'}, dimensions={0} | all-to-all | bytes 6291456 | tf_op jit(solution)/shard_map/all_to_all | solution.py:21
  162.1 4.7 %copy.28 = bf16[1536,4,256]{0,2,1:T(8,128)(2,1)} copy(bf16[1536,4,256]{2,0,1:T(8,128)(2,1)} %bitcast.41) | data formatting | bytes 6291456 | tf_op jit(solution)/shard_map/all_to_all | solution.py:21
  166.8 12.0 %reduce-scatter.3.cloned.1.call-done = f32[768,256]{0,1:T(8,128)} async-done(((f32[768,1024]{0,1:T(8,128)}), f32[768,256]{0,1:T(8,128)}) %reduce-scatter.3.cloned.1.call-update) | async-done | bytes 786448 | tf_op jit(solution)/shard_map/reduce_scatter | solution.py:28
  178.8 1.2 negate_convert_fusion
  180.0 1.0 convolution_bitcast_fusion.2
  181.0 0.0 all-reduce.5.cloned.1.call-update
  181.0 0.0 reduce-scatter.5.cloned.1.call-start
  181.0 6.2 %convolution_bitcast_fusion = f32[768,1024]{0,1:T(8,128)} fusion(bf16[1536,1024]{0,1:T(8,128)(2,1)} %bitcast.44, bf16[768,1536]{1,0:T(8,128)(2,1)S(1)} %copy-done), kind=kOutput, calls=%fused_computation | convolution fusion | flops 2415919104 | bytes 8650752 | tf_op jit(solution)/shard_map/dot_general | solution.py:27
  187.3 0.0 reduce-scatter.5.cloned.1.call-update
  187.3 0.0 all-gather.8.cloned.1.call-start
  187.4 0.5 all-gather.8.cloned.1.call-update
  187.9 0.0 all-reduce.7.cloned.1.call-start
  187.9 1.1 copy.27
  189.0 0.6 dynamic_slice.17
  190.3 0.9 copy.31
  191.2 26.0 %all-reduce.5.cloned.1.call-done = f32[256,256]{0,1:T(8,128)} async-done(((f32[256,256]{0,1:T(8,128)}), f32[256,256]{0,1:T(8,128)}) %all-reduce.5.cloned.1.call-update) | async-done | bytes 262160 | tf_op jit(solution)/shard_map/psum | solution.py:49
  217.2 0.0 all-reduce.9.cloned.1.call-start
  217.3 46.6 %reduce-scatter.5.cloned.1.call-done = f32[768,256]{0,1:T(8,128)} async-done(((f32[768,1024]{0,1:T(8,128)}), f32[768,256]{0,1:T(8,128)}) %reduce-scatter.5.cloned.1.call-update) | async-done | bytes 786448 | tf_op jit(solution)/shard_map/reduce_scatter | solution.py:28
  263.8 32.6 %all-gather.8.cloned.1.call-done = bf16[768,1024]{0,1:T(8,128)(2,1)} async-done(((bf16[768,256]{0,1:T(8,128)(2,1)}), bf16[768,1024]{0,1:T(8,128)(2,1)}) %all-gather.8.cloned.1.call-update) | async-done | bytes 1572880 | tf_op jit(solution)/shard_map/all_gather | solution.py:54
  296.4 1.6 fusion.1
  298.0 2.0 fusion.6
  300.0 1.0 fusion.13
  301.0 0.0 all-reduce.9.cloned.1.call-update
  301.0 16.0 %all-reduce.7.cloned.1.call-done = f32[256,256]{0,1:T(8,128)} async-done(((f32[256,256]{0,1:T(8,128)}), f32[256,256]{0,1:T(8,128)}) %all-reduce.7.cloned.1.call-update) | async-done | bytes 262160 | tf_op jit(solution)/shard_map/psum | solution.py:49
  317.0 1.0 subtract_convert_fusion
  318.0 0.8 copy.32
  318.7 11.7 %all_gather.15 = bf16[256,1024]{0,1:T(8,128)(2,1)} all-gather(bf16[256,256]{0,1:T(8,128)(2,1)S(1)} %subtract_convert_fusion), channel_id=1, replica_groups=mesh['grp'=2,'row'=4,'col'=4] {'col'}, dimensions={1}, use_global_device_ids=true | all-gather | bytes 655360 | tf_op jit(solution)/shard_map/all_gather | solution.py:55
  330.4 0.9 copy.33
  331.3 45.8 %all-reduce.9.cloned.1.call-done = (f32[256,256]{1,0:T(8,128)}, f32[256,256]{1,0:T(8,128)}) async-done(((f32[256,256]{1,0:T(8,128)}, f32[256,256]{1,0:T(8,128)}), (f32[256,256]{1,0:T(8,128)}, f32[256,256]{1,0:T(8,128)})) %all-reduce.9.cloned.1.call-update) | async-done | bytes 524304 | tf_op jit(solution)/shard_map/psum | solution.py:71
  377.0 1.2 fusion.5
  378.3 2.0 fusion.4
  (19 shorter events, 0.1 us)
Async XLA Ops:
  7.2 91.4 %copy-start = (bf16[768,1536]{1,0:T(8,128)(2,1)S(1)}, bf16[768,1536]{1,0:T(8,128)(2,1)}, u32[]{:S(2)}) copy-start(bf16[768,1536]{1,0:T(8,128)(2,1)} %param.9) | copy-start | bytes 7077892
  7.2 44.1 %all-gather.4.cloned.1.call-start = ((), (), s32[]{:S(2)}) async-start(), calls=%async_computation.4 | async-start | bytes 3538944 | tf_op jit(solution)/shard_map/all_gather | solution.py:20
  10.2 94.6 %all-gather.6.cloned.1.call-start = ((), (), s32[]{:S(2)}) async-start(), calls=%async_computation.8 | async-start | bytes 3538944 | tf_op jit(solution)/shard_map/all_gather | solution.py:20
  12.3 166.5 %reduce-scatter.3.cloned.1.call-start = ((), (), s32[]{:S(2)}) async-start(), calls=%async_computation.5 | async-start | bytes 3932160 | tf_op jit(solution)/shard_map/reduce_scatter | solution.py:28
  104.8 112.4 %all-reduce.5.cloned.1.call-start = ((), (), s32[]{:S(2)}) async-start(), calls=%async_computation.6 | async-start | bytes 524288 | tf_op jit(solution)/shard_map/psum | solution.py:49
  162.1 17.9 %copy-start.4 = (bf16[768,256]{1,0:T(8,128)(2,1)S(1)}, bf16[768,256]{1,0:T(8,128)(2,1)}, u32[]{:S(2)}) copy-start(bf16[768,256]{1,0:T(8,128)(2,1)} %broadcast_select_fusion.1) | copy-start | bytes 1179652
  180.0 7.3 %copy-start.2 = (bf16[768,256]{0,1:T(8,128)(2,1)}, bf16[768,256]{0,1:T(8,128)(2,1)S(1)}, u32[]{:S(2)}) copy-start(bf16[768,256]{0,1:T(8,128)(2,1)S(1)} %negate_convert_fusion) | copy-start | bytes 1179652
  181.0 82.8 %reduce-scatter.5.cloned.1.call-start = ((), (), s32[]{:S(2)}) async-start(), calls=%async_computation.9 | async-start | bytes 3932160 | tf_op jit(solution)/shard_map/reduce_scatter | solution.py:28
  187.3 1.8 copy-start.7
  187.3 109.1 %copy-start.5 = (bf16[256,256]{1,0:T(8,128)(2,1)S(1)}, bf16[256,256]{1,0:T(8,128)(2,1)}, u32[]{:S(2)}) copy-start(bf16[256,256]{1,0:T(8,128)(2,1)} %param.16) | copy-start | bytes 393220
  187.3 3.0 copy-start.3
  187.3 110.7 %copy-start.1 = (bf16[768,256]{1,0:T(8,128)(2,1)S(1)}, bf16[768,256]{1,0:T(8,128)(2,1)}, u32[]{:S(2)}) copy-start(bf16[768,256]{1,0:T(8,128)(2,1)} %broadcast_select_fusion) | copy-start | bytes 1179652
  187.3 109.1 %all-gather.8.cloned.1.call-start = ((), (), s32[]{:S(2)}) async-start(), calls=%async_computation.10 | async-start | bytes 1966080 | tf_op jit(solution)/shard_map/all_gather | solution.py:54
  187.9 129.1 %all-reduce.7.cloned.1.call-start = ((), (), s32[]{:S(2)}) async-start(), calls=%async_computation.7 | async-start | bytes 524288 | tf_op jit(solution)/shard_map/psum | solution.py:49
  217.2 159.8 %all-reduce.9.cloned.1.call-start = ((), (), s32[]{:S(2)}) async-start(), calls=%async_computation.11 | async-start | bytes 1048576 | tf_op jit(solution)/shard_map/psum | solution.py:71
  378.3 2.0 copy-start.6
Sparse Core Ops, SparseCore 0:
  10.3 40.9 all-gather.3
  52.9 37.1 all-gather.5
  104.9 73.8 reduce-scatter.2
  181.6 35.5 all-reduce.4
  220.0 43.7 reduce-scatter.4
  265.5 30.8 all-gather.7
  298.7 18.2 all-reduce.6
  319.3 57.6 all-reduce.8
